TPU v7x, 256 devices: a whole 4x4x8 slice. The times are simulated.
256 devices in a mesh: section: 8 (over z), expert: 32 (over x, y, core).
Axes of the slice: x: 4, y: 4, z: 8, core: 2. Of those that a mesh axis runs over, the one named last changes fastest.
Arguments:
- tokens: bfloat16 [4, 4, 512, 1024], P(None, None, 'expert'), may hold values from -6 to 6
- expert_ids: int32 [8, 4, 4, 512, 2], P('section', None, None, 'expert'), may hold values from 0 to 7, as said below
- router_weight: float32 [8, 4, 1024, 8], P('section'), may hold values from -0.375 to 0.375
- w_gate: bfloat16 [8, 32, 1024, 1792], P('section', 'expert'), may hold values from -0.1875 to 0.1875
- w_up: bfloat16 [8, 32, 1024, 1792], P('section', 'expert'), may hold values from -0.1875 to 0.1875
- w_down: bfloat16 [8, 32, 1792, 1024], P('section', 'expert'), may hold values from -0.125 to 0.125
Outputs:
- layer_outputs: bfloat16 [8, 4, 4, 512, 1024], P('section', None, None, 'expert')
Inputs may be any that keep to these rules, and one draw needn't show every extreme that they name: `expert_ids`: the two entries of a token are different experts. In each aligned block of 8 tokens (same layer, micro-batch and replica) no expert is named by more than 4 tokens, and some expert by exactly 4.
All inputs are finite; a program needn't handle non-finite values.
Results may differ from a plain program's by a relative error of at most 0.02.
Values may be sent and summed in bfloat16 or wider, within the bound.
A program may use at most 64 MiB of HBM per device.

v0:
```python
import jax
import jax.numpy as jnp
from jax import lax
from jax.sharding import PartitionSpec as P

EXPERTS = 8
CAP = 4


def shifted(array, axis, by):
    peers = lax.axis_size(axis)
    pairs = [(i, i + by) for i in range(peers) if 0 <= i + by < peers]
    return lax.ppermute(array, axis, pairs)


def prepare(current, routes, router_mat, capacity):
    replicas, tok_rows, width = current.shape
    values = current.astype(jnp.float32)
    normed = (values * lax.rsqrt(jnp.mean(values * values, axis=-1, keepdims=True) + 1e-06)).astype(
        jnp.bfloat16
    )
    logits = jnp.einsum(
        "rtd,rde->rte", normed.astype(jnp.float32), router_mat, precision=lax.Precision.HIGHEST
    )
    scores = jax.nn.sigmoid(logits)
    expert_range = jnp.arange(EXPERTS, dtype=jnp.int32)
    matches = routes[..., None] == expert_range
    picked = jnp.sum(jnp.where(matches, scores[:, :, None, :], 0.0), axis=-1)
    gates = picked / jnp.sum(picked, axis=-1, keepdims=True)
    flat_ids = routes.reshape(replicas, tok_rows * 2)
    one_hot = (flat_ids[..., None] == expert_range).astype(jnp.int32)
    earlier = jnp.cumsum(one_hot, axis=1) - one_hot
    position = jnp.sum(earlier * one_hot, axis=-1)
    target = flat_ids * capacity + position
    slot_range = jnp.arange(EXPERTS * capacity, dtype=jnp.int32)
    placing = jnp.sum(
        (
            target.reshape(replicas, tok_rows, 2)[:, None, :, :] == slot_range[None, :, None, None]
        ).astype(jnp.int32),
        axis=-1,
    ).astype(jnp.bfloat16)
    outgoing = jnp.einsum(
        "rst,rtd->rsd", placing, normed, preferred_element_type=jnp.float32
    ).astype(jnp.bfloat16)
    outgoing = outgoing.reshape(replicas * EXPERTS, capacity, width)
    return (gates, target, outgoing)


def compute(received, weights, active_flag):
    gate_mat, up_mat, down_mat = weights
    width = received.shape[2]
    total_rows = received.shape[0] * received.shape[1]
    flat_rows = received.reshape(total_rows, width)

    def working(inputs):
        gate_val = jnp.dot(inputs, gate_mat, preferred_element_type=jnp.float32)
        up_val = jnp.dot(inputs, up_mat, preferred_element_type=jnp.float32)
        inner = (jax.nn.silu(gate_val) * up_val).astype(jnp.bfloat16)
        return jnp.dot(inner, down_mat, preferred_element_type=jnp.float32).astype(jnp.bfloat16)

    def resting(inputs):
        return jnp.zeros((total_rows, width), jnp.bfloat16)

    return lax.cond(active_flag, working, resting, flat_rows).reshape(received.shape)


def send_out(outgoing, serve):
    return serve(lax.all_to_all(outgoing, "expert", split_axis=0, concat_axis=0, tiled=True))


def combine(current, gates, target, answers, capacity):
    replicas, tok_rows, width = current.shape
    values = current.astype(jnp.float32)
    answers = answers.reshape(replicas, EXPERTS * capacity, width)
    gathered = answers[jnp.arange(replicas, dtype=jnp.int32)[:, None], target]
    weighted = gathered.reshape(replicas, tok_rows, 2, width).astype(jnp.float32) * gates[..., None]
    return (values + jnp.sum(weighted, axis=2)).astype(jnp.bfloat16)


def per_device(tokens, expert_ids, router_weight, w_gate, w_up, w_down):
    batches, replicas, tok_dev, width = tokens.shape
    section_count = lax.axis_size("section")
    section_index = lax.axis_index("section")
    pieces = 1
    capacity = 2 * CAP
    tok_rows = tok_dev // pieces
    unit_total = batches * pieces
    weights = (w_gate[0, 0], w_up[0, 0], w_down[0, 0])
    router_mat = router_weight[0]
    routes_all = expert_ids[0]
    zero_index = jnp.zeros((), jnp.int32)

    def locate(unit_now):
        clipped = jnp.clip(unit_now, 0, unit_total - 1)
        batch_now = clipped // pieces
        offset = clipped % pieces * tok_rows
        return (batch_now, offset)

    def store_rows(stored, result, unit_now):
        valid = jnp.logical_and(unit_now >= 0, unit_now < unit_total)
        batch_now, offset = locate(unit_now)
        updated = lax.dynamic_update_slice(
            stored, result[None], (batch_now, zero_index, offset, zero_index)
        )
        return jnp.where(valid, updated, stored)

    def inputs_for(unit_now):
        batch_now, offset = locate(unit_now)
        fresh = lax.dynamic_slice(
            tokens, (batch_now, zero_index, offset, zero_index), (1, replicas, tok_rows, width)
        )[0]
        routes = lax.dynamic_slice(
            routes_all, (batch_now, zero_index, offset, zero_index), (1, replicas, tok_rows, 2)
        )[0]
        return (fresh, routes)

    stored_start = jnp.zeros((batches, replicas, tok_dev, width), jnp.bfloat16)

    def advance(step_now, carry):
        previous, stored = carry
        incoming = shifted(previous, "section", 1)
        unit_now = step_now - section_index
        active_flag = jnp.logical_and(unit_now >= 0, unit_now < unit_total)
        fresh, routes = inputs_for(unit_now)
        current = jnp.where(section_index == 0, fresh, incoming)
        gates, target, outgoing = prepare(current, routes, router_mat, capacity)

        def serve(received):
            results = compute(received, weights, active_flag)
            return lax.all_to_all(results, "expert", split_axis=0, concat_axis=0, tiled=True)

        answers = send_out(outgoing, serve)
        result = combine(current, gates, target, answers, capacity)
        return (result, store_rows(stored, result, unit_now))

    start = (jnp.zeros((replicas, tok_rows, width), jnp.bfloat16), stored_start)
    finished = lax.fori_loop(0, unit_total + section_count - 1, advance, start)
    return finished[1][None]


def solution(mesh):
    in_specs = (
        P(None, None, "expert", None),
        P("section", None, None, "expert", None),
        P("section", None, None, None),
        P("section", "expert", None, None),
        P("section", "expert", None, None),
        P("section", "expert", None, None),
    )
    out_specs = P("section", None, None, "expert", None)
    return jax.shard_map(
        per_device, mesh=mesh, in_specs=in_specs, out_specs=out_specs, check_vma=False
    )
```

profile of v0, /device:TPU:231, one launch (start us, length us, event | category | flops | bytes accessed | tf_op | source)
XLA Modules:
  0.0 574.1 jit_solution(13302369932132049848)
XLA Ops:
  0.9 572.4 %while.18 = (s32[]{:T(128)}, bf16[4,16,1024]{2,1,0:T(8,128)(2,1)S(1)}, bf16[4,4,16,1024]{3,2,1,0:T(8,128)(2,1)S(1)}, pred[]{:T(512)}, s32[]{:T(128)}, /*index=5*...) while((s32[]{:T(128)}, ...), condition=%wide.region_10.11_spmd.clone, body=%wide.region_0.10_spmd.clone.sunk | while | flops 2837779456 | bytes 24979600 | solution.py:137
  9.4 8.7 %all-to-all-start = ((bf16[32,8,1024]{2,1,0:T(8,128)(2,1)}), bf16[32,8,1024]{2,1,0:T(8,128)(2,1)S(1)}, u32[]{:S(2)}, u32[]{:S(2)}) async-start(bf16[32,8,1024]{2,1,0:T(8,128)(2,1)} %bitcast.50), calls=%async_computation | async-start | bytes 1048576 | tf_op jit(solution)/shard_map/while/body/eval_jaxpr/all_to_all | solution.py:68
  18.4 9.4 %all-to-all-done = bf16[32,8,1024]{2,1,0:T(8,128)(2,1)S(1)} async-done(((bf16[32,8,1024]{2,1,0:T(8,128)(2,1)}), bf16[32,8,1024]{2,1,0:T(8,128)(2,1)S(1)}, u32[]{:S(2)}, u32[]{:S(2)}) %all-to-all-start) | async-done | bytes 524320 | tf_op jit(solution)/shard_map/while/body/eval_jaxpr/all_to_all | solution.py:68
  34.7 9.2 %all-to-all-done.1 = bf16[32,8,1024]{2,1,0:T(8,128)(2,1)S(1)} async-done(((bf16[32,8,1024]{2,1,0:T(8,128)(2,1)}), bf16[32,8,1024]{2,1,0:T(8,128)(2,1)S(1)}, u32[]{:S(2)}, u32[]{:S(2)}) %all-to-all-start.1) | async-done | bytes 524320 | tf_op jit(solution)/shard_map/while/body/eval_jaxpr/all_to_all | solution.py:130
  62.6 9.4 %all-to-all-done = bf16[32,8,1024]{2,1,0:T(8,128)(2,1)S(1)} async-done(((bf16[32,8,1024]{2,1,0:T(8,128)(2,1)}), bf16[32,8,1024]{2,1,0:T(8,128)(2,1)S(1)}, u32[]{:S(2)}, u32[]{:S(2)}) %all-to-all-start) | async-done | bytes 524320 | tf_op jit(solution)/shard_map/while/body/eval_jaxpr/all_to_all | solution.py:68
  78.8 9.2 %all-to-all-done.1 = bf16[32,8,1024]{2,1,0:T(8,128)(2,1)S(1)} async-done(((bf16[32,8,1024]{2,1,0:T(8,128)(2,1)}), bf16[32,8,1024]{2,1,0:T(8,128)(2,1)S(1)}, u32[]{:S(2)}, u32[]{:S(2)}) %all-to-all-start.1) | async-done | bytes 524320 | tf_op jit(solution)/shard_map/while/body/eval_jaxpr/all_to_all | solution.py:130
  106.7 9.4 %all-to-all-done = bf16[32,8,1024]{2,1,0:T(8,128)(2,1)S(1)} async-done(((bf16[32,8,1024]{2,1,0:T(8,128)(2,1)}), bf16[32,8,1024]{2,1,0:T(8,128)(2,1)S(1)}, u32[]{:S(2)}, u32[]{:S(2)}) %all-to-all-start) | async-done | bytes 524320 | tf_op jit(solution)/shard_map/while/body/eval_jaxpr/all_to_all | solution.py:68
  123.0 9.2 %all-to-all-done.1 = bf16[32,8,1024]{2,1,0:T(8,128)(2,1)S(1)} async-done(((bf16[32,8,1024]{2,1,0:T(8,128)(2,1)}), bf16[32,8,1024]{2,1,0:T(8,128)(2,1)S(1)}, u32[]{:S(2)}, u32[]{:S(2)}) %all-to-all-start.1) | async-done | bytes 524320 | tf_op jit(solution)/shard_map/while/body/eval_jaxpr/all_to_all | solution.py:130
  150.8 9.4 %all-to-all-done = bf16[32,8,1024]{2,1,0:T(8,128)(2,1)S(1)} async-done(((bf16[32,8,1024]{2,1,0:T(8,128)(2,1)}), bf16[32,8,1024]{2,1,0:T(8,128)(2,1)S(1)}, u32[]{:S(2)}, u32[]{:S(2)}) %all-to-all-start) | async-done | bytes 524320 | tf_op jit(solution)/shard_map/while/body/eval_jaxpr/all_to_all | solution.py:68
  167.1 9.2 %all-to-all-done.1 = bf16[32,8,1024]{2,1,0:T(8,128)(2,1)S(1)} async-done(((bf16[32,8,1024]{2,1,0:T(8,128)(2,1)}), bf16[32,8,1024]{2,1,0:T(8,128)(2,1)S(1)}, u32[]{:S(2)}, u32[]{:S(2)}) %all-to-all-start.1) | async-done | bytes 524320 | tf_op jit(solution)/shard_map/while/body/eval_jaxpr/all_to_all | solution.py:130
  195.0 9.4 %all-to-all-done = bf16[32,8,1024]{2,1,0:T(8,128)(2,1)S(1)} async-done(((bf16[32,8,1024]{2,1,0:T(8,128)(2,1)}), bf16[32,8,1024]{2,1,0:T(8,128)(2,1)S(1)}, u32[]{:S(2)}, u32[]{:S(2)}) %all-to-all-start) | async-done | bytes 524320 | tf_op jit(solution)/shard_map/while/body/eval_jaxpr/all_to_all | solution.py:68
  211.2 9.2 %all-to-all-done.1 = bf16[32,8,1024]{2,1,0:T(8,128)(2,1)S(1)} async-done(((bf16[32,8,1024]{2,1,0:T(8,128)(2,1)}), bf16[32,8,1024]{2,1,0:T(8,128)(2,1)S(1)}, u32[]{:S(2)}, u32[]{:S(2)}) %all-to-all-start.1) | async-done | bytes 524320 | tf_op jit(solution)/shard_map/while/body/eval_jaxpr/all_to_all | solution.py:130
  239.9 9.4 %all-to-all-done = bf16[32,8,1024]{2,1,0:T(8,128)(2,1)S(1)} async-done(((bf16[32,8,1024]{2,1,0:T(8,128)(2,1)}), bf16[32,8,1024]{2,1,0:T(8,128)(2,1)S(1)}, u32[]{:S(2)}, u32[]{:S(2)}) %all-to-all-start) | async-done | bytes 524320 | tf_op jit(solution)/shard_map/while/body/eval_jaxpr/all_to_all | solution.py:68
  256.1 9.2 %all-to-all-done.1 = bf16[32,8,1024]{2,1,0:T(8,128)(2,1)S(1)} async-done(((bf16[32,8,1024]{2,1,0:T(8,128)(2,1)}), bf16[32,8,1024]{2,1,0:T(8,128)(2,1)S(1)}, u32[]{:S(2)}, u32[]{:S(2)}) %all-to-all-start.1) | async-done | bytes 524320 | tf_op jit(solution)/shard_map/while/body/eval_jaxpr/all_to_all | solution.py:130
  285.2 9.4 %all-to-all-done = bf16[32,8,1024]{2,1,0:T(8,128)(2,1)S(1)} async-done(((bf16[32,8,1024]{2,1,0:T(8,128)(2,1)}), bf16[32,8,1024]{2,1,0:T(8,128)(2,1)S(1)}, u32[]{:S(2)}, u32[]{:S(2)}) %all-to-all-start) | async-done | bytes 524320 | tf_op jit(solution)/shard_map/while/body/eval_jaxpr/all_to_all | solution.py:68
  301.5 9.2 %all-to-all-done.1 = bf16[32,8,1024]{2,1,0:T(8,128)(2,1)S(1)} async-done(((bf16[32,8,1024]{2,1,0:T(8,128)(2,1)}), bf16[32,8,1024]{2,1,0:T(8,128)(2,1)S(1)}, u32[]{:S(2)}, u32[]{:S(2)}) %all-to-all-start.1) | async-done | bytes 524320 | tf_op jit(solution)/shard_map/while/body/eval_jaxpr/all_to_all | solution.py:130
  315.7 51.1 %collective-permute-done = bf16[4,16,1024]{2,1,0:T(8,128)(2,1)S(1)} collective-permute-done((bf16[4,16,1024]{2,1,0:T(8,128)(2,1)S(1)}, bf16[4,16,1024]{2,1,0:T(8,128)(2,1)S(1)}, u32[]{:S(2)}, u32[]{:S(2)}) %collective-permute-start) | collective-permute-done | bytes 131104 | tf_op jit(solution)/shard_map/while/body/eval_jaxpr/ppermute | solution.py:13
  375.2 9.4 %all-to-all-done = bf16[32,8,1024]{2,1,0:T(8,128)(2,1)S(1)} async-done(((bf16[32,8,1024]{2,1,0:T(8,128)(2,1)}), bf16[32,8,1024]{2,1,0:T(8,128)(2,1)S(1)}, u32[]{:S(2)}, u32[]{:S(2)}) %all-to-all-start) | async-done | bytes 524320 | tf_op jit(solution)/shard_map/while/body/eval_jaxpr/all_to_all | solution.py:68
  384.6 9.3 %conditional.3 = (bf16[256,1024]{1,0:T(8,128)(2,1)}) conditional(s32[]{:T(128)} %convert_element_type.163, () %tuple.62, (bf16[32,8,1024]{2,1,0:T(8,128)(2,1)S(1)}, bf16[1024,1792]{1,0:T(8,128)(2,1)}, bf16[1024,1792]{1,0:T(8,128)(2,1)}, bf16[1792,1024]{1,0:T(8,128)(2,1)}) %tuple.63), branch_computations={%region_5.5_spmd, %region_6.6_spmd} | conditional | flops 2821586944 | bytes 16252936 | solution.py:64
  399.9 9.2 %all-to-all-done.1 = bf16[32,8,1024]{2,1,0:T(8,128)(2,1)S(1)} async-done(((bf16[32,8,1024]{2,1,0:T(8,128)(2,1)}), bf16[32,8,1024]{2,1,0:T(8,128)(2,1)S(1)}, u32[]{:S(2)}, u32[]{:S(2)}) %all-to-all-start.1) | async-done | bytes 524320 | tf_op jit(solution)/shard_map/while/body/eval_jaxpr/all_to_all | solution.py:130
  414.2 6.4 %collective-permute-done = bf16[4,16,1024]{2,1,0:T(8,128)(2,1)S(1)} collective-permute-done((bf16[4,16,1024]{2,1,0:T(8,128)(2,1)S(1)}, bf16[4,16,1024]{2,1,0:T(8,128)(2,1)S(1)}, u32[]{:S(2)}, u32[]{:S(2)}) %collective-permute-start) | collective-permute-done | bytes 131104 | tf_op jit(solution)/shard_map/while/body/eval_jaxpr/ppermute | solution.py:13
  429.0 9.4 %all-to-all-done = bf16[32,8,1024]{2,1,0:T(8,128)(2,1)S(1)} async-done(((bf16[32,8,1024]{2,1,0:T(8,128)(2,1)}), bf16[32,8,1024]{2,1,0:T(8,128)(2,1)S(1)}, u32[]{:S(2)}, u32[]{:S(2)}) %all-to-all-start) | async-done | bytes 524320 | tf_op jit(solution)/shard_map/while/body/eval_jaxpr/all_to_all | solution.py:68
  438.4 9.3 %conditional.3 = (bf16[256,1024]{1,0:T(8,128)(2,1)}) conditional(s32[]{:T(128)} %convert_element_type.163, () %tuple.62, (bf16[32,8,1024]{2,1,0:T(8,128)(2,1)S(1)}, bf16[1024,1792]{1,0:T(8,128)(2,1)}, bf16[1024,1792]{1,0:T(8,128)(2,1)}, bf16[1792,1024]{1,0:T(8,128)(2,1)}) %tuple.63), branch_computations={%region_5.5_spmd, %region_6.6_spmd} | conditional | flops 2821586944 | bytes 16252936 | solution.py:64
  453.7 9.2 %all-to-all-done.1 = bf16[32,8,1024]{2,1,0:T(8,128)(2,1)S(1)} async-done(((bf16[32,8,1024]{2,1,0:T(8,128)(2,1)}), bf16[32,8,1024]{2,1,0:T(8,128)(2,1)S(1)}, u32[]{:S(2)}, u32[]{:S(2)}) %all-to-all-start.1) | async-done | bytes 524320 | tf_op jit(solution)/shard_map/while/body/eval_jaxpr/all_to_all | solution.py:130
  468.0 6.4 %collective-permute-done = bf16[4,16,1024]{2,1,0:T(8,128)(2,1)S(1)} collective-permute-done((bf16[4,16,1024]{2,1,0:T(8,128)(2,1)S(1)}, bf16[4,16,1024]{2,1,0:T(8,128)(2,1)S(1)}, u32[]{:S(2)}, u32[]{:S(2)}) %collective-permute-start) | collective-permute-done | bytes 131104 | tf_op jit(solution)/shard_map/while/body/eval_jaxpr/ppermute | solution.py:13
  482.8 9.4 %all-to-all-done = bf16[32,8,1024]{2,1,0:T(8,128)(2,1)S(1)} async-done(((bf16[32,8,1024]{2,1,0:T(8,128)(2,1)}), bf16[32,8,1024]{2,1,0:T(8,128)(2,1)S(1)}, u32[]{:S(2)}, u32[]{:S(2)}) %all-to-all-start) | async-done | bytes 524320 | tf_op jit(solution)/shard_map/while/body/eval_jaxpr/all_to_all | solution.py:68
  492.2 9.3 %conditional.3 = (bf16[256,1024]{1,0:T(8,128)(2,1)}) conditional(s32[]{:T(128)} %convert_element_type.163, () %tuple.62, (bf16[32,8,1024]{2,1,0:T(8,128)(2,1)S(1)}, bf16[1024,1792]{1,0:T(8,128)(2,1)}, bf16[1024,1792]{1,0:T(8,128)(2,1)}, bf16[1792,1024]{1,0:T(8,128)(2,1)}) %tuple.63), branch_computations={%region_5.5_spmd, %region_6.6_spmd} | conditional | flops 2821586944 | bytes 16252936 | solution.py:64
  507.5 9.2 %all-to-all-done.1 = bf16[32,8,1024]{2,1,0:T(8,128)(2,1)S(1)} async-done(((bf16[32,8,1024]{2,1,0:T(8,128)(2,1)}), bf16[32,8,1024]{2,1,0:T(8,128)(2,1)S(1)}, u32[]{:S(2)}, u32[]{:S(2)}) %all-to-all-start.1) | async-done | bytes 524320 | tf_op jit(solution)/shard_map/while/body/eval_jaxpr/all_to_all | solution.py:130
  521.7 6.4 %collective-permute-done = bf16[4,16,1024]{2,1,0:T(8,128)(2,1)S(1)} collective-permute-done((bf16[4,16,1024]{2,1,0:T(8,128)(2,1)S(1)}, bf16[4,16,1024]{2,1,0:T(8,128)(2,1)S(1)}, u32[]{:S(2)}, u32[]{:S(2)}) %collective-permute-start) | collective-permute-done | bytes 131104 | tf_op jit(solution)/shard_map/while/body/eval_jaxpr/ppermute | solution.py:13
  536.6 9.4 %all-to-all-done = bf16[32,8,1024]{2,1,0:T(8,128)(2,1)S(1)} async-done(((bf16[32,8,1024]{2,1,0:T(8,128)(2,1)}), bf16[32,8,1024]{2,1,0:T(8,128)(2,1)S(1)}, u32[]{:S(2)}, u32[]{:S(2)}) %all-to-all-start) | async-done | bytes 524320 | tf_op jit(solution)/shard_map/while/body/eval_jaxpr/all_to_all | solution.py:68
  546.0 9.3 %conditional.3 = (bf16[256,1024]{1,0:T(8,128)(2,1)}) conditional(s32[]{:T(128)} %convert_element_type.163, () %tuple.62, (bf16[32,8,1024]{2,1,0:T(8,128)(2,1)S(1)}, bf16[1024,1792]{1,0:T(8,128)(2,1)}, bf16[1024,1792]{1,0:T(8,128)(2,1)}, bf16[1792,1024]{1,0:T(8,128)(2,1)}) %tuple.63), branch_computations={%region_5.5_spmd, %region_6.6_spmd} | conditional | flops 2821586944 | bytes 16252936 | solution.py:64
  561.3 9.2 %all-to-all-done.1 = bf16[32,8,1024]{2,1,0:T(8,128)(2,1)S(1)} async-done(((bf16[32,8,1024]{2,1,0:T(8,128)(2,1)}), bf16[32,8,1024]{2,1,0:T(8,128)(2,1)S(1)}, u32[]{:S(2)}, u32[]{:S(2)}) %all-to-all-start.1) | async-done | bytes 524320 | tf_op jit(solution)/shard_map/while/body/eval_jaxpr/all_to_all | solution.py:130
  (396 shorter events, 294.9 us)
Async XLA Ops:
  9.4 18.4 %all-to-all-start = ((bf16[32,8,1024]{2,1,0:T(8,128)(2,1)}), bf16[32,8,1024]{2,1,0:T(8,128)(2,1)S(1)}, u32[]{:S(2)}, u32[]{:S(2)}) async-start(bf16[32,8,1024]{2,1,0:T(8,128)(2,1)} %bitcast.50), calls=%async_computation | async-start | bytes 1048576 | tf_op jit(solution)/shard_map/while/body/eval_jaxpr/all_to_all | solution.py:68
  28.7 15.2 %all-to-all-start.1 = ((bf16[32,8,1024]{2,1,0:T(8,128)(2,1)}), bf16[32,8,1024]{2,1,0:T(8,128)(2,1)S(1)}, u32[]{:S(2)}, u32[]{:S(2)}) async-start(bf16[32,8,1024]{2,1,0:T(8,128)(2,1)} %bitcast.51), calls=%async_computation.1 | async-start | bytes 1048576 | tf_op jit(solution)/shard_map/while/body/eval_jaxpr/all_to_all | solution.py:130
  46.7 7.0 %collective-permute-start = (bf16[4,16,1024]{2,1,0:T(8,128)(2,1)S(1)}, bf16[4,16,1024]{2,1,0:T(8,128)(2,1)S(1)}, u32[]{:S(2)}, u32[]{:S(2)}) collective-permute-start(bf16[4,16,1024]{2,1,0:T(8,128)(2,1)S(1)} %broadcast_select_fusion.2), channel_id=1, source_target_pairs={{0,32},{32,64},{64,96},{96,128},{128,160},{160,192},{192,224},{1,3... | collective-permute-start | bytes 393224 | tf_op jit(solution)/shard_map/while/body/eval_jaxpr/ppermute | solution.py:13
  55.9 16.1 %all-to-all-start = ((bf16[32,8,1024]{2,1,0:T(8,128)(2,1)}), bf16[32,8,1024]{2,1,0:T(8,128)(2,1)S(1)}, u32[]{:S(2)}, u32[]{:S(2)}) async-start(bf16[32,8,1024]{2,1,0:T(8,128)(2,1)} %bitcast.50), calls=%async_computation | async-start | bytes 1048576 | tf_op jit(solution)/shard_map/while/body/eval_jaxpr/all_to_all | solution.py:68
  72.8 15.2 %all-to-all-start.1 = ((bf16[32,8,1024]{2,1,0:T(8,128)(2,1)}), bf16[32,8,1024]{2,1,0:T(8,128)(2,1)S(1)}, u32[]{:S(2)}, u32[]{:S(2)}) async-start(bf16[32,8,1024]{2,1,0:T(8,128)(2,1)} %bitcast.51), calls=%async_computation.1 | async-start | bytes 1048576 | tf_op jit(solution)/shard_map/while/body/eval_jaxpr/all_to_all | solution.py:130
  90.9 7.0 %collective-permute-start = (bf16[4,16,1024]{2,1,0:T(8,128)(2,1)S(1)}, bf16[4,16,1024]{2,1,0:T(8,128)(2,1)S(1)}, u32[]{:S(2)}, u32[]{:S(2)}) collective-permute-start(bf16[4,16,1024]{2,1,0:T(8,128)(2,1)S(1)} %broadcast_select_fusion.2), channel_id=1, source_target_pairs={{0,32},{32,64},{64,96},{96,128},{128,160},{160,192},{192,224},{1,3... | collective-permute-start | bytes 393224 | tf_op jit(solution)/shard_map/while/body/eval_jaxpr/ppermute | solution.py:13
  100.0 16.1 %all-to-all-start = ((bf16[32,8,1024]{2,1,0:T(8,128)(2,1)}), bf16[32,8,1024]{2,1,0:T(8,128)(2,1)S(1)}, u32[]{:S(2)}, u32[]{:S(2)}) async-start(bf16[32,8,1024]{2,1,0:T(8,128)(2,1)} %bitcast.50), calls=%async_computation | async-start | bytes 1048576 | tf_op jit(solution)/shard_map/while/body/eval_jaxpr/all_to_all | solution.py:68
  116.9 15.2 %all-to-all-start.1 = ((bf16[32,8,1024]{2,1,0:T(8,128)(2,1)}), bf16[32,8,1024]{2,1,0:T(8,128)(2,1)S(1)}, u32[]{:S(2)}, u32[]{:S(2)}) async-start(bf16[32,8,1024]{2,1,0:T(8,128)(2,1)} %bitcast.51), calls=%async_computation.1 | async-start | bytes 1048576 | tf_op jit(solution)/shard_map/while/body/eval_jaxpr/all_to_all | solution.py:130
  135.0 7.0 %collective-permute-start = (bf16[4,16,1024]{2,1,0:T(8,128)(2,1)S(1)}, bf16[4,16,1024]{2,1,0:T(8,128)(2,1)S(1)}, u32[]{:S(2)}, u32[]{:S(2)}) collective-permute-start(bf16[4,16,1024]{2,1,0:T(8,128)(2,1)S(1)} %broadcast_select_fusion.2), channel_id=1, source_target_pairs={{0,32},{32,64},{64,96},{96,128},{128,160},{160,192},{192,224},{1,3... | collective-permute-start | bytes 393224 | tf_op jit(solution)/shard_map/while/body/eval_jaxpr/ppermute | solution.py:13
  144.1 16.1 %all-to-all-start = ((bf16[32,8,1024]{2,1,0:T(8,128)(2,1)}), bf16[32,8,1024]{2,1,0:T(8,128)(2,1)S(1)}, u32[]{:S(2)}, u32[]{:S(2)}) async-start(bf16[32,8,1024]{2,1,0:T(8,128)(2,1)} %bitcast.50), calls=%async_computation | async-start | bytes 1048576 | tf_op jit(solution)/shard_map/while/body/eval_jaxpr/all_to_all | solution.py:68
  161.1 15.2 %all-to-all-start.1 = ((bf16[32,8,1024]{2,1,0:T(8,128)(2,1)}), bf16[32,8,1024]{2,1,0:T(8,128)(2,1)S(1)}, u32[]{:S(2)}, u32[]{:S(2)}) async-start(bf16[32,8,1024]{2,1,0:T(8,128)(2,1)} %bitcast.51), calls=%async_computation.1 | async-start | bytes 1048576 | tf_op jit(solution)/shard_map/while/body/eval_jaxpr/all_to_all | solution.py:130
  179.1 7.0 %collective-permute-start = (bf16[4,16,1024]{2,1,0:T(8,128)(2,1)S(1)}, bf16[4,16,1024]{2,1,0:T(8,128)(2,1)S(1)}, u32[]{:S(2)}, u32[]{:S(2)}) collective-permute-start(bf16[4,16,1024]{2,1,0:T(8,128)(2,1)S(1)} %broadcast_select_fusion.2), channel_id=1, source_target_pairs={{0,32},{32,64},{64,96},{96,128},{128,160},{160,192},{192,224},{1,3... | collective-permute-start | bytes 393224 | tf_op jit(solution)/shard_map/while/body/eval_jaxpr/ppermute | solution.py:13
  188.2 16.1 %all-to-all-start = ((bf16[32,8,1024]{2,1,0:T(8,128)(2,1)}), bf16[32,8,1024]{2,1,0:T(8,128)(2,1)S(1)}, u32[]{:S(2)}, u32[]{:S(2)}) async-start(bf16[32,8,1024]{2,1,0:T(8,128)(2,1)} %bitcast.50), calls=%async_computation | async-start | bytes 1048576 | tf_op jit(solution)/shard_map/while/body/eval_jaxpr/all_to_all | solution.py:68
  205.2 15.2 %all-to-all-start.1 = ((bf16[32,8,1024]{2,1,0:T(8,128)(2,1)}), bf16[32,8,1024]{2,1,0:T(8,128)(2,1)S(1)}, u32[]{:S(2)}, u32[]{:S(2)}) async-start(bf16[32,8,1024]{2,1,0:T(8,128)(2,1)} %bitcast.51), calls=%async_computation.1 | async-start | bytes 1048576 | tf_op jit(solution)/shard_map/while/body/eval_jaxpr/all_to_all | solution.py:130
  223.2 8.3 %collective-permute-start = (bf16[4,16,1024]{2,1,0:T(8,128)(2,1)S(1)}, bf16[4,16,1024]{2,1,0:T(8,128)(2,1)S(1)}, u32[]{:S(2)}, u32[]{:S(2)}) collective-permute-start(bf16[4,16,1024]{2,1,0:T(8,128)(2,1)S(1)} %broadcast_select_fusion.2), channel_id=1, source_target_pairs={{0,32},{32,64},{64,96},{96,128},{128,160},{160,192},{192,224},{1,3... | collective-permute-start | bytes 393224 | tf_op jit(solution)/shard_map/while/body/eval_jaxpr/ppermute | solution.py:13
  233.7 15.6 %all-to-all-start = ((bf16[32,8,1024]{2,1,0:T(8,128)(2,1)}), bf16[32,8,1024]{2,1,0:T(8,128)(2,1)S(1)}, u32[]{:S(2)}, u32[]{:S(2)}) async-start(bf16[32,8,1024]{2,1,0:T(8,128)(2,1)} %bitcast.50), calls=%async_computation | async-start | bytes 1048576 | tf_op jit(solution)/shard_map/while/body/eval_jaxpr/all_to_all | solution.py:68
  250.1 15.2 %all-to-all-start.1 = ((bf16[32,8,1024]{2,1,0:T(8,128)(2,1)}), bf16[32,8,1024]{2,1,0:T(8,128)(2,1)S(1)}, u32[]{:S(2)}, u32[]{:S(2)}) async-start(bf16[32,8,1024]{2,1,0:T(8,128)(2,1)} %bitcast.51), calls=%async_computation.1 | async-start | bytes 1048576 | tf_op jit(solution)/shard_map/while/body/eval_jaxpr/all_to_all | solution.py:130
  268.2 8.6 %collective-permute-start = (bf16[4,16,1024]{2,1,0:T(8,128)(2,1)S(1)}, bf16[4,16,1024]{2,1,0:T(8,128)(2,1)S(1)}, u32[]{:S(2)}, u32[]{:S(2)}) collective-permute-start(bf16[4,16,1024]{2,1,0:T(8,128)(2,1)S(1)} %broadcast_select_fusion.2), channel_id=1, source_target_pairs={{0,32},{32,64},{64,96},{96,128},{128,160},{160,192},{192,224},{1,3... | collective-permute-start | bytes 393224 | tf_op jit(solution)/shard_map/while/body/eval_jaxpr/ppermute | solution.py:13
  279.0 15.6 %all-to-all-start = ((bf16[32,8,1024]{2,1,0:T(8,128)(2,1)}), bf16[32,8,1024]{2,1,0:T(8,128)(2,1)S(1)}, u32[]{:S(2)}, u32[]{:S(2)}) async-start(bf16[32,8,1024]{2,1,0:T(8,128)(2,1)} %bitcast.50), calls=%async_computation | async-start | bytes 1048576 | tf_op jit(solution)/shard_map/while/body/eval_jaxpr/all_to_all | solution.py:68
  295.4 15.2 %all-to-all-start.1 = ((bf16[32,8,1024]{2,1,0:T(8,128)(2,1)}), bf16[32,8,1024]{2,1,0:T(8,128)(2,1)S(1)}, u32[]{:S(2)}, u32[]{:S(2)}) async-start(bf16[32,8,1024]{2,1,0:T(8,128)(2,1)} %bitcast.51), calls=%async_computation.1 | async-start | bytes 1048576 | tf_op jit(solution)/shard_map/while/body/eval_jaxpr/all_to_all | solution.py:130
  313.5 53.3 %collective-permute-start = (bf16[4,16,1024]{2,1,0:T(8,128)(2,1)S(1)}, bf16[4,16,1024]{2,1,0:T(8,128)(2,1)S(1)}, u32[]{:S(2)}, u32[]{:S(2)}) collective-permute-start(bf16[4,16,1024]{2,1,0:T(8,128)(2,1)S(1)} %broadcast_select_fusion.2), channel_id=1, source_target_pairs={{0,32},{32,64},{64,96},{96,128},{128,160},{160,192},{192,224},{1,3... | collective-permute-start | bytes 393224 | tf_op jit(solution)/shard_map/while/body/eval_jaxpr/ppermute | solution.py:13
  369.0 15.6 %all-to-all-start = ((bf16[32,8,1024]{2,1,0:T(8,128)(2,1)}), bf16[32,8,1024]{2,1,0:T(8,128)(2,1)S(1)}, u32[]{:S(2)}, u32[]{:S(2)}) async-start(bf16[32,8,1024]{2,1,0:T(8,128)(2,1)} %bitcast.50), calls=%async_computation | async-start | bytes 1048576 | tf_op jit(solution)/shard_map/while/body/eval_jaxpr/all_to_all | solution.py:68
  393.9 15.2 %all-to-all-start.1 = ((bf16[32,8,1024]{2,1,0:T(8,128)(2,1)}), bf16[32,8,1024]{2,1,0:T(8,128)(2,1)S(1)}, u32[]{:S(2)}, u32[]{:S(2)}) async-start(bf16[32,8,1024]{2,1,0:T(8,128)(2,1)} %bitcast.51), calls=%async_computation.1 | async-start | bytes 1048576 | tf_op jit(solution)/shard_map/while/body/eval_jaxpr/all_to_all | solution.py:130
  412.0 8.6 %collective-permute-start = (bf16[4,16,1024]{2,1,0:T(8,128)(2,1)S(1)}, bf16[4,16,1024]{2,1,0:T(8,128)(2,1)S(1)}, u32[]{:S(2)}, u32[]{:S(2)}) collective-permute-start(bf16[4,16,1024]{2,1,0:T(8,128)(2,1)S(1)} %broadcast_select_fusion.2), channel_id=1, source_target_pairs={{0,32},{32,64},{64,96},{96,128},{128,160},{160,192},{192,224},{1,3... | collective-permute-start | bytes 393224 | tf_op jit(solution)/shard_map/while/body/eval_jaxpr/ppermute | solution.py:13
  422.8 15.6 %all-to-all-start = ((bf16[32,8,1024]{2,1,0:T(8,128)(2,1)}), bf16[32,8,1024]{2,1,0:T(8,128)(2,1)S(1)}, u32[]{:S(2)}, u32[]{:S(2)}) async-start(bf16[32,8,1024]{2,1,0:T(8,128)(2,1)} %bitcast.50), calls=%async_computation | async-start | bytes 1048576 | tf_op jit(solution)/shard_map/while/body/eval_jaxpr/all_to_all | solution.py:68
  447.7 15.2 %all-to-all-start.1 = ((bf16[32,8,1024]{2,1,0:T(8,128)(2,1)}), bf16[32,8,1024]{2,1,0:T(8,128)(2,1)S(1)}, u32[]{:S(2)}, u32[]{:S(2)}) async-start(bf16[32,8,1024]{2,1,0:T(8,128)(2,1)} %bitcast.51), calls=%async_computation.1 | async-start | bytes 1048576 | tf_op jit(solution)/shard_map/while/body/eval_jaxpr/all_to_all | solution.py:130
  465.8 8.6 %collective-permute-start = (bf16[4,16,1024]{2,1,0:T(8,128)(2,1)S(1)}, bf16[4,16,1024]{2,1,0:T(8,128)(2,1)S(1)}, u32[]{:S(2)}, u32[]{:S(2)}) collective-permute-start(bf16[4,16,1024]{2,1,0:T(8,128)(2,1)S(1)} %broadcast_select_fusion.2), channel_id=1, source_target_pairs={{0,32},{32,64},{64,96},{96,128},{128,160},{160,192},{192,224},{1,3... | collective-permute-start | bytes 393224 | tf_op jit(solution)/shard_map/while/body/eval_jaxpr/ppermute | solution.py:13
  476.6 15.6 %all-to-all-start = ((bf16[32,8,1024]{2,1,0:T(8,128)(2,1)}), bf16[32,8,1024]{2,1,0:T(8,128)(2,1)S(1)}, u32[]{:S(2)}, u32[]{:S(2)}) async-start(bf16[32,8,1024]{2,1,0:T(8,128)(2,1)} %bitcast.50), calls=%async_computation | async-start | bytes 1048576 | tf_op jit(solution)/shard_map/while/body/eval_jaxpr/all_to_all | solution.py:68
  501.5 15.2 %all-to-all-start.1 = ((bf16[32,8,1024]{2,1,0:T(8,128)(2,1)}), bf16[32,8,1024]{2,1,0:T(8,128)(2,1)S(1)}, u32[]{:S(2)}, u32[]{:S(2)}) async-start(bf16[32,8,1024]{2,1,0:T(8,128)(2,1)} %bitcast.51), calls=%async_computation.1 | async-start | bytes 1048576 | tf_op jit(solution)/shard_map/while/body/eval_jaxpr/all_to_all | solution.py:130
  519.5 8.6 %collective-permute-start = (bf16[4,16,1024]{2,1,0:T(8,128)(2,1)S(1)}, bf16[4,16,1024]{2,1,0:T(8,128)(2,1)S(1)}, u32[]{:S(2)}, u32[]{:S(2)}) collective-permute-start(bf16[4,16,1024]{2,1,0:T(8,128)(2,1)S(1)} %broadcast_select_fusion.2), channel_id=1, source_target_pairs={{0,32},{32,64},{64,96},{96,128},{128,160},{160,192},{192,224},{1,3... | collective-permute-start | bytes 393224 | tf_op jit(solution)/shard_map/while/body/eval_jaxpr/ppermute | solution.py:13
  530.4 15.6 %all-to-all-start = ((bf16[32,8,1024]{2,1,0:T(8,128)(2,1)}), bf16[32,8,1024]{2,1,0:T(8,128)(2,1)S(1)}, u32[]{:S(2)}, u32[]{:S(2)}) async-start(bf16[32,8,1024]{2,1,0:T(8,128)(2,1)} %bitcast.50), calls=%async_computation | async-start | bytes 1048576 | tf_op jit(solution)/shard_map/while/body/eval_jaxpr/all_to_all | solution.py:68
  555.3 15.2 %all-to-all-start.1 = ((bf16[32,8,1024]{2,1,0:T(8,128)(2,1)}), bf16[32,8,1024]{2,1,0:T(8,128)(2,1)S(1)}, u32[]{:S(2)}, u32[]{:S(2)}) async-start(bf16[32,8,1024]{2,1,0:T(8,128)(2,1)} %bitcast.51), calls=%async_computation.1 | async-start | bytes 1048576 | tf_op jit(solution)/shard_map/while/body/eval_jaxpr/all_to_all | solution.py:130
  (13 other events, 111.4 us)
where the time goes:
time: 579 us; the launch traced here: 574 us
  waiting for transfers between devices  310 us (54%)
  starting transfers between devices  145 us (25%)
  matrix products  53.3 us (9%)
  local copies, waits for them, and re-layouts  37.4 us (6%)
  other arithmetic  26.1 us (5%)
    ppermute x11, waiting for transfers between devices, shifted(): return lax.ppermute(array, axis, pairs)  106 us
    all_to_all x11, waiting for transfers between devices, send_out(): lax.all_to_all(outgoing, 'expert', split_axis=0, concat_axis=0, tiled=True)  103 us
    all_to_all x11, waiting for transfers between devices, serve(): lax.all_to_all(results, 'expert', split_axis=0, concat_axis=0, tiled=True)  101 us
    all_to_all x11, starting transfers between devices, send_out(): lax.all_to_all(outgoing, 'expert', split_axis=0, concat_axis=0, tiled=True)  70.1 us
    all_to_all x11, starting transfers between devices, serve(): lax.all_to_all(results, 'expert', split_axis=0, concat_axis=0, tiled=True)  60.9 us
    dot_general x4, matrix products, working(): jnp.dot(inner, down_mat, preferred_element_type=jnp.float32)  24.5 us
    gather x11, local copies, waits for them, and re-layouts, combine(): gathered = answers[jnp.arange(replicas, dtype=jnp.int32)[:, None], target]  18.2 us
    ppermute x11, starting transfers between devices, shifted(): return lax.ppermute(array, axis, pairs)  14.2 us
  transfers between devices with their start and end apart: 33, of which 33 were waited for; matrix products, arithmetic and copies ran while one was open for 3% of the time, Pallas kernels for 0%

commit v1 on v0

v1 whole, which is shorter than its diff:
```python
import functools

import jax
import jax.numpy as jnp
from jax import lax
from jax.experimental import pallas as pl
from jax.experimental.pallas import tpu as pltpu
from jax.sharding import PartitionSpec as P

CAP = 4
BLOCK = 8
GROUPS = 2
TILE = 256
MESH = pl.DeviceIdType.MESH
F32 = jnp.float32
BF16 = jnp.bfloat16


def slot_columns(routes, place, slots):
    micro, reps, tok, top = routes.shape
    blocks = tok // BLOCK
    flat = routes.reshape(micro, reps, blocks, BLOCK * top)
    order = jnp.arange(BLOCK * top, dtype=jnp.int32)
    same = (flat[..., :, None] == flat[..., None, :]) & (order[None, :] < order[:, None])
    position = jnp.sum(same.astype(jnp.int32), axis=-1)
    block = place * blocks + jnp.arange(blocks, dtype=jnp.int32)
    columns = flat * slots + block[None, None, :, None] * CAP + position
    columns = columns.reshape(micro, reps, tok, top)
    return jnp.pad(jnp.swapaxes(columns, 0, 1), ((0, 0), (0, 0), (0, 0), (0, 128 - top)))


def router_parts(router, slots):
    parts, rest = [], router
    for _ in range(3):
        part = lax.reduce_precision(rest, 8, 7)
        rest = rest - part
        parts.append(jnp.repeat(part.astype(BF16), slots, axis=1))
    return jnp.concatenate(parts, axis=1)


def pipeline(
    sizes,
    tokens_ref,
    codes_ref,
    router_ref,
    gate_hbm,
    up_hbm,
    down_hbm,
    out_ref,
    w_gate,
    w_up,
    w_down,
    held,
    codes,
    gates,
    slot_send,
    slot_recv,
    inner,
    back_send,
    back_recv,
    result,
    weight_sem,
    code_sem,
    code_send_sem,
    token_send_sem,
    held_sem,
    slot_sem,
    slot_send_sem,
    back_sem,
    back_send_sem,
    next_send_sem,
    out_sem,
    out_send_sem,
):
    sections, experts, reps, micro, tok, width, hidden = sizes
    pieces = reps // GROUPS
    units = micro * pieces
    slots = GROUPS * tok // 2
    rows = experts * slots
    section = lax.axis_index("section")
    index = lax.axis_index("expert")
    column = index // experts
    mine = index % experts

    weights = [
        pltpu.make_async_copy(gate_hbm, w_gate, weight_sem.at[0]),
        pltpu.make_async_copy(up_hbm, w_up, weight_sem.at[1]),
        pltpu.make_async_copy(down_hbm, w_down, weight_sem.at[2]),
    ]
    for copy in weights:
        copy.start()

    barrier = pltpu.get_barrier_semaphore()

    def greet(at_section, at_index):
        pl.semaphore_signal(
            barrier, inc=1, device_id=(at_section, at_index), device_id_type=MESH
        )

    for step in range(1, experts):
        greet(section, column * experts + (mine + step) % experts)
    for step in range(1, reps):
        greet(section, (column + step) % reps * experts + mine)

    @pl.when(section > 0)
    def _():
        greet(section - 1, index)

    @pl.when(section < sections - 1)
    def _():
        greet(section + 1, index)

    below = jnp.where(section > 0, 1, 0)
    above = jnp.where(section < sections - 1, 1, 0)
    pl.semaphore_wait(barrier, experts - 1 + reps - 1 + below + above)

    @pl.when(section == 0)
    def _():
        for batch in range(micro):
            unit = batch * pieces + column // GROUPS
            place = pl.ds(column % GROUPS * tok, tok)
            for step in range(1, reps):
                rep = (column + step) % reps
                pltpu.make_async_remote_copy(
                    src_ref=tokens_ref.at[batch, rep],
                    dst_ref=held.at[unit, place],
                    send_sem=token_send_sem,
                    recv_sem=held_sem.at[unit],
                    device_id=(section, rep * experts + mine),
                    device_id_type=MESH,
                ).start()
            pltpu.make_async_copy(
                tokens_ref.at[batch, column], held.at[unit, place], held_sem.at[unit]
            ).start()

    for step in range(1, reps):
        rep = (column + step) % reps
        pltpu.make_async_remote_copy(
            src_ref=codes_ref.at[rep],
            dst_ref=codes.at[column],
            send_sem=code_send_sem,
            recv_sem=code_sem,
            device_id=(section, rep * experts + mine),
            device_id_type=MESH,
        ).start()
    pltpu.make_async_copy(codes_ref.at[column], codes.at[column], code_sem).start()
    pltpu.make_async_copy(codes_ref, codes, code_sem).wait()

    lanes = lax.broadcasted_iota(jnp.int32, (GROUPS * tok, rows), 1)

    def prepare(unit):
        pltpu.make_async_copy(held.at[unit], held.at[unit], held_sem.at[unit]).wait()
        values = held[unit].astype(F32)
        scale = lax.rsqrt(jnp.mean(values * values, axis=-1, keepdims=True) + 1e-06)
        normed = (values * scale).astype(BF16)
        logits = jnp.dot(normed, router_ref[...], preferred_element_type=F32)
        logits = (logits[:, :rows] + logits[:, rows : 2 * rows]) + logits[:, 2 * rows :]
        batch, piece = unit // pieces, unit % pieces
        code = jnp.concatenate(
            [codes[piece * GROUPS + group, batch] for group in range(GROUPS)], axis=0
        )
        chosen = (code[:, 0:1] == lanes) | (code[:, 1:2] == lanes)
        picked = jnp.where(chosen, jax.nn.sigmoid(logits), 0.0)
        gates[unit] = picked / jnp.sum(picked, axis=-1, keepdims=True)
        placing = jnp.where(chosen, 1.0, 0.0).astype(BF16)
        filled = lax.dot_general(
            placing, normed, (((0,), (0,)), ((), ())), preferred_element_type=F32
        )
        slot_send[unit] = filled.astype(BF16).reshape(experts, slots, width)
        slot_recv[unit, mine] = slot_send[unit, mine]
        for step in range(1, experts):
            peer = (mine + step) % experts
            pltpu.make_async_remote_copy(
                src_ref=slot_send.at[unit, peer],
                dst_ref=slot_recv.at[unit, mine],
                send_sem=slot_send_sem,
                recv_sem=slot_sem.at[unit],
                device_id=(section, column * experts + peer),
                device_id_type=MESH,
            ).start()

    def serve(unit):
        @pl.when(unit == 0)
        def _():
            for copy in weights:
                copy.wait()

        others = slot_recv.at[unit, pl.ds(0, experts - 1)]
        pltpu.make_async_copy(others, others, slot_sem.at[unit]).wait()
        given = slot_recv[unit].reshape(rows, width)
        for tile in range(hidden // TILE):
            part = slice(tile * TILE, (tile + 1) * TILE)
            gate_val = jnp.dot(given, w_gate[:, part], preferred_element_type=F32)
            up_val = jnp.dot(given, w_up[:, part], preferred_element_type=F32)
            inner[:, part] = (jax.nn.silu(gate_val) * up_val).astype(BF16)
        for tile in range(width // TILE):
            part = slice(tile * TILE, (tile + 1) * TILE)
            answer = jnp.dot(inner[...], w_down[:, part], preferred_element_type=F32)
            back_send[unit, :, :, part] = answer.astype(BF16).reshape(experts, slots, TILE)
        back_recv[unit, mine] = back_send[unit, mine]
        for step in range(1, experts):
            peer = (mine + step) % experts
            pltpu.make_async_remote_copy(
                src_ref=back_send.at[unit, peer],
                dst_ref=back_recv.at[unit, mine],
                send_sem=back_send_sem,
                recv_sem=back_sem.at[unit],
                device_id=(section, column * experts + peer),
                device_id_type=MESH,
            ).start()

    def combine(unit):
        others = back_recv.at[unit, pl.ds(0, experts - 1)]
        pltpu.make_async_copy(others, others, back_sem.at[unit]).wait()
        answers = back_recv[unit].reshape(rows, width)
        weight = gates[unit]
        high = weight.astype(BF16)
        low = (weight - high.astype(F32)).astype(BF16)
        total = jnp.dot(high, answers, preferred_element_type=F32)
        total = total + jnp.dot(low, answers, preferred_element_type=F32)
        result[unit] = (held[unit].astype(F32) + total).astype(BF16)

        @pl.when(section < sections - 1)
        def _():
            pltpu.make_async_remote_copy(
                src_ref=result.at[unit],
                dst_ref=held.at[unit],
                send_sem=next_send_sem,
                recv_sem=held_sem.at[unit],
                device_id=(section + 1, index),
                device_id_type=MESH,
            ).start()

        batch, piece = unit // pieces, unit % pieces
        for group in range(GROUPS):
            owner = piece * GROUPS + group
            source = result.at[unit, pl.ds(group * tok, tok)]
            target = out_ref.at[0, batch, column]

            @pl.when(owner == column)
            def _():
                pltpu.make_async_copy(source, target, out_sem).start()

            @pl.when(owner != column)
            def _():
                pltpu.make_async_remote_copy(
                    src_ref=source,
                    dst_ref=target,
                    send_sem=out_send_sem,
                    recv_sem=out_sem,
                    device_id=(section, owner * experts + mine),
                    device_id_type=MESH,
                ).start()

    def tick(now, carry):
        @pl.when(now < units)
        def _():
            prepare(now)

        @pl.when(jnp.logical_and(now >= 1, now < units + 1))
        def _():
            serve(now - 1)

        @pl.when(now >= 2)
        def _():
            combine(now - 2)

        return carry

    lax.fori_loop(0, units + 2, tick, 0)

    def drain(ref, sem):
        pltpu.make_async_copy(ref, ref, sem).wait()

    drain(codes.at[pl.ds(0, reps - 1)], code_send_sem)
    drain(slot_send.at[:, pl.ds(0, experts - 1)], slot_send_sem)
    drain(back_send.at[:, pl.ds(0, experts - 1)], back_send_sem)

    @pl.when(section == 0)
    def _():
        drain(out_ref.at[0, :, pl.ds(0, reps - 1)], token_send_sem)

    @pl.when(section < sections - 1)
    def _():
        drain(result, next_send_sem)

    drain(out_ref.at[0, :, pl.ds(0, reps - 1)], out_send_sem)
    drain(out_ref, out_sem)


def per_device(tokens, expert_ids, router_weight, w_gate, w_up, w_down):
    micro, reps, tok, width = tokens.shape
    hidden = w_gate.shape[3]
    sections = lax.axis_size("section")
    experts = lax.axis_size("expert") // reps
    units = micro * reps // GROUPS
    unit_rows = GROUPS * tok
    slots = unit_rows // 2
    rows = experts * slots
    column = lax.axis_index("expert") // experts
    codes = slot_columns(expert_ids[0], column % GROUPS, slots)
    router = router_parts(
        lax.dynamic_index_in_dim(router_weight[0], column, 0, keepdims=False), slots
    )
    sizes = (sections, experts, reps, micro, tok, width, hidden)
    anywhere = pl.BlockSpec(memory_space=pl.ANY)
    local = pl.BlockSpec(memory_space=pltpu.VMEM)
    dma = pltpu.SemaphoreType.DMA
    exchange = pltpu.VMEM((units, experts, slots, width), BF16)
    return pl.pallas_call(
        functools.partial(pipeline, sizes),
        out_shape=jax.ShapeDtypeStruct((1, micro, reps, tok, width), BF16),
        in_specs=[anywhere, anywhere, local, anywhere, anywhere, anywhere],
        out_specs=anywhere,
        scratch_shapes=[
            pltpu.VMEM((width, hidden), BF16),
            pltpu.VMEM((width, hidden), BF16),
            pltpu.VMEM((hidden, width), BF16),
            pltpu.VMEM((units, unit_rows, width), BF16),
            pltpu.VMEM((reps, micro, tok, 128), jnp.int32),
            pltpu.VMEM((units, unit_rows, rows), F32),
            exchange,
            exchange,
            pltpu.VMEM((rows, hidden), BF16),
            exchange,
            exchange,
            pltpu.VMEM((units, unit_rows, width), BF16),
            dma((3,)),
            dma,
            dma,
            dma,
            dma((units,)),
            dma((units,)),
            dma,
            dma((units,)),
            dma,
            dma,
            dma,
            dma,
        ],
        compiler_params=pltpu.CompilerParams(
            collective_id=0, has_side_effects=True, vmem_limit_bytes=52 * 1024 * 1024
        ),
    )(tokens, codes, router, w_gate[0, 0], w_up[0, 0], w_down[0, 0])


def solution(mesh):
    in_specs = (
        P(None, None, "expert", None),
        P("section", None, None, "expert", None),
        P("section", None, None, None),
        P("section", "expert", None, None),
        P("section", "expert", None, None),
        P("section", "expert", None, None),
    )
    out_specs = P("section", None, None, "expert", None)
    return jax.shard_map(
        per_device, mesh=mesh, in_specs=in_specs, out_specs=out_specs, check_vma=False
    )
```

time: 579 us -> 197 us (0.34)
  waiting for transfers between devices: 310 us -> 0 us
  Pallas kernels: 0 us -> 192 us
  starting transfers between devices: 145 us -> 0 us
  matrix products: 53.3 us -> 0 us
  local copies, waits for them, and re-layouts: 37.4 us -> 2.66 us
  other arithmetic: 26.1 us -> 1.74 us
    all_to_all x22 -> x0, waiting for transfers between devices: 204 us -> none  [the longest x11 103 us: send_out(): lax.all_to_all(outgoing, 'expert', split_axis=0, concat_axis=0, tiled=True)]
    pallas_call x0 -> x1, Pallas kernels: none -> 192 us  [per_device(): pl.pallas_call(functools.partial(pipeline, sizes), out_shape=jax.ShapeDty...]
    all_to_all x22 -> x0, starting transfers between devices: 131 us -> none  [the longest x11 70.1 us: send_out(): lax.all_to_all(outgoing, 'expert', split_axis=0, concat_axis=0, tiled=True)]
    ppermute x11 -> x0, waiting for transfers between devices: 106 us -> none  [shifted(): return lax.ppermute(array, axis, pairs)]
    dot_general x30 -> x0, matrix products: 53.3 us -> none  [the longest x4 24.5 us: working(): jnp.dot(inner, down_mat, preferred_element_type=jnp.float32)]
    reduce_sum x55 -> x1, other arithmetic: 22.9 us -> 0.77 us  [slot_columns(): position = jnp.sum(same.astype(jnp.int32), axis=-1)]
    gather x11 -> x0, local copies, waits for them, and re-layouts: 18.2 us -> none  [combine(): gathered = answers[jnp.arange(replicas, dtype=jnp.int32)[:, None], target]]
    ppermute x11 -> x0, starting transfers between devices: 14.2 us -> none  [shifted(): return lax.ppermute(array, axis, pairs)]
  transfers between devices with their start and end apart: 33 -> 0, of which waited for: 33 -> 0; matrix products, arithmetic and copies ran while one was open for 3% -> 0% of each run, Pallas kernels for 0% -> 0%
where the time goes in v1:
time: 197 us
  Pallas kernels  192 us (97%)
  local copies, waits for them, and re-layouts  2.66 us (1%)
    pallas_call x1, Pallas kernels, per_device(): pl.pallas_call(functools.partial(pipeline, sizes), out_shape=jax.ShapeDty...  192 us

profile of v1, /device:TPU:231, one launch (start us, length us, event | category | flops | bytes accessed | tf_op | source)
XLA Modules:
  0.0 196.8 jit_solution(7914926814590005572)
XLA Ops:
  0.0 0.8 reduce-precision_convert_fusion.1
  0.8 0.2 copy.22
  1.0 0.0 copy-start.1
  1.0 0.2 copy.23
  1.2 0.2 copy.24
  1.4 0.0 copy-start
  1.4 0.1 pad_maximum_fusion.router_ref
  1.6 0.1 add.41
  1.6 0.1 add.42
  1.7 0.0 copy-done.1
  1.7 0.1 copy.17
  1.8 0.1 copy.18
  2.0 0.8 convert_reduce_fusion
  2.7 0.1 copy.20
  2.9 0.6 copy.21
  3.4 0.2 copy.16
  3.6 0.1 fusion.1
  3.7 0.0 copy-done
  3.7 192.3 %shard_map.64 = bf16[1,4,4,16,1024]{4,3,2,1,0:T(8,128)(2,1)S(1)} custom-call(bf16[4,4,16,1024]{3,2,1,0:T(8,128)(2,1)S(1)} %copy-done, s32[4,4,16,128]{3,2,1,0:T(8,128)S(1)} %pad.4.codes_ref, bf16[1024,384]{1,0:T(8,128)(2,1)S(1)} %pad_maximum_fusion.router_ref, bf16[1024,1792]{1,0:T(8,128)(2,1)} %bitcast.23, bf16[1024,1792]{1,0:T(8,128)(2,1)} %bitcast.24, ...), custom_call_target="tpu_custom_call" | custom-call | tf_op jit(solution)/shard_map/pallas_call | solution.py:310
  196.0 0.8 copy.26
  (6 shorter events, 0.1 us)
Async XLA Ops:
  1.0 0.7 copy-start.1
  1.4 2.3 %copy-start = (bf16[4,4,16,1024]{3,2,1,0:T(8,128)(2,1)S(1)}, bf16[4,4,16,1024]{3,2,1,0:T(8,128)(2,1)}, u32[]{:S(2)}) copy-start(bf16[4,4,16,1024]{3,2,1,0:T(8,128)(2,1)} %tokens_ref.1) | copy-start | bytes 1572868

commit v2 on v1

v2 whole, which is shorter than its diff:
```python
import functools

import jax
import jax.numpy as jnp
from jax import lax
from jax.experimental import pallas as pl
from jax.experimental.pallas import tpu as pltpu
from jax.sharding import PartitionSpec as P

CAP = 4
BLOCK = 8
SERVE = 1
COMBINE = 2
TILE = 256
PARTS = 2
MESH = pl.DeviceIdType.MESH
F32 = jnp.float32
BF16 = jnp.bfloat16


def chosen_lanes(routes):
    micro, reps, tok, top = routes.shape
    named = jnp.transpose(routes, (1, 2, 0, 3)).reshape(reps, tok, micro * top)
    return jnp.pad(named.astype(F32), ((0, 0), (0, 0), (0, 128 - micro * top)))


def pipeline(
    sizes,
    tokens_ref,
    routes_ref,
    router_ref,
    gate_hbm,
    up_hbm,
    down_hbm,
    out_ref,
    w_gate,
    w_up,
    w_down,
    held,
    routes,
    router_raw,
    router,
    gates,
    slot_send,
    slot_recv,
    inner,
    back_send,
    back_recv,
    result,
    weight_sem,
    router_sem,
    route_sem,
    route_send_sem,
    token_send_sem,
    held_sem,
    slot_sem,
    slot_send_sem,
    back_sem,
    back_send_sem,
    next_send_sem,
    out_sem,
    out_send_sem,
):
    sections, experts, reps, micro, tok, width, hidden = sizes
    units = micro * reps
    slots = tok // 2
    rows = experts * slots
    section = lax.axis_index("section")
    index = lax.axis_index("expert")
    column = index // experts
    mine = index % experts
    far_first = sorted(range(1, experts), key=lambda step: -min(step, experts - step))

    router_copy = pltpu.make_async_copy(router_ref.at[column], router_raw, router_sem)
    router_copy.start()
    weights = [
        pltpu.make_async_copy(gate_hbm, w_gate, weight_sem.at[0]),
        pltpu.make_async_copy(up_hbm, w_up, weight_sem.at[1]),
        pltpu.make_async_copy(down_hbm, w_down, weight_sem.at[2]),
    ]
    barrier = pltpu.get_barrier_semaphore()

    def greet(at_section, at_index):
        pl.semaphore_signal(
            barrier, inc=1, device_id=(at_section, at_index), device_id_type=MESH
        )

    for step in range(1, experts):
        greet(section, column * experts + (mine + step) % experts)
    for step in range(1, reps):
        greet(section, (column + step) % reps * experts + mine)

    @pl.when(section > 0)
    def _():
        greet(section - 1, index)

    @pl.when(section < sections - 1)
    def _():
        greet(section + 1, index)

    below = jnp.where(section > 0, 1, 0)
    above = jnp.where(section < sections - 1, 1, 0)
    pl.semaphore_wait(barrier, experts - 1 + reps - 1 + below + above)

    def spread_tokens(batch):
        unit = batch * reps + column
        for step in range(1, reps):
            rep = (column + step) % reps
            pltpu.make_async_remote_copy(
                src_ref=tokens_ref.at[batch, rep],
                dst_ref=held.at[unit],
                send_sem=token_send_sem,
                recv_sem=held_sem.at[unit],
                device_id=(section, rep * experts + mine),
                device_id_type=MESH,
            ).start()
        pltpu.make_async_copy(
            tokens_ref.at[batch, column], held.at[unit], held_sem.at[unit]
        ).start()

    @pl.when(section == 0)
    def _():
        spread_tokens(0)

    for step in range(1, reps):
        rep = (column + step) % reps
        pltpu.make_async_remote_copy(
            src_ref=routes_ref.at[rep],
            dst_ref=routes.at[column],
            send_sem=route_send_sem,
            recv_sem=route_sem,
            device_id=(section, rep * experts + mine),
            device_id_type=MESH,
        ).start()

    @pl.when(section == 0)
    def _():
        for batch in range(1, micro):
            spread_tokens(batch)

    for copy in weights:
        copy.start()

    routes[column] = routes_ref[column]
    router_copy.wait()
    shift = slots.bit_length() - 1
    spread = lax.broadcasted_iota(jnp.int32, (rows, experts), 1) == jnp.right_shift(
        lax.broadcasted_iota(jnp.int32, (rows, experts), 0), shift
    )
    spread = jnp.where(spread, 1.0, 0.0).astype(BF16)
    rest = router_raw[...]
    for part in range(3):
        piece = rest.astype(BF16)
        rest = rest - piece.astype(F32)
        router[part * rows : (part + 1) * rows, :] = jnp.dot(
            spread, piece, preferred_element_type=F32
        ).astype(BF16)

    lanes = lax.broadcasted_iota(jnp.int32, (tok, 128), 1)
    columns = lax.broadcasted_iota(jnp.int32, (tok, rows), 1)
    expert_lane = jnp.right_shift(columns, shift).astype(F32)
    block_row = jnp.right_shift(lax.broadcasted_iota(jnp.int32, (tok, rows), 0), 3)
    rank_lane = (jnp.bitwise_and(columns, slots - 1) - block_row * CAP).astype(F32)
    row = lax.broadcasted_iota(jnp.int32, (tok, tok), 0)
    earlier = lax.broadcasted_iota(jnp.int32, (tok, tok), 1)
    earlier = (earlier < row) & (jnp.right_shift(earlier, 3) == jnp.right_shift(row, 3))
    earlier = jnp.where(earlier, 1.0, 0.0).astype(BF16)

    others = routes.at[pl.ds(0, reps - 1)]
    pltpu.make_async_copy(others, others, route_sem).wait()

    def prepare(unit):
        batch, origin = unit // reps, unit % reps
        route = routes[origin]
        first = jnp.sum(jnp.where(lanes == 2 * batch, route, 0.0), axis=-1, keepdims=True)
        second = jnp.sum(jnp.where(lanes == 2 * batch + 1, route, 0.0), axis=-1, keepdims=True)
        named = (first == expert_lane) | (second == expert_lane)
        rank = jnp.dot(
            earlier, jnp.where(named, 1.0, 0.0).astype(BF16), preferred_element_type=F32
        )
        chosen = jnp.where(named & (rank == rank_lane), 1.0, 0.0)
        placing = chosen.astype(BF16)

        pltpu.make_async_copy(held.at[unit], held.at[unit], held_sem.at[unit]).wait()
        values = held[unit].astype(F32)
        scale = lax.rsqrt(jnp.mean(values * values, axis=-1, keepdims=True) + 1e-06)
        normed = (values * scale).astype(BF16)
        filled = lax.dot_general(
            placing, normed, (((0,), (0,)), ((), ())), preferred_element_type=F32
        )
        slot_send[unit] = filled.astype(BF16).reshape(experts, slots, width)
        for step in far_first:
            peer = (mine + step) % experts
            pltpu.make_async_remote_copy(
                src_ref=slot_send.at[unit, peer],
                dst_ref=slot_recv.at[unit, mine],
                send_sem=slot_send_sem,
                recv_sem=slot_sem.at[unit],
                device_id=(section, column * experts + peer),
                device_id_type=MESH,
            ).start()
        slot_recv[unit, mine] = slot_send[unit, mine]
        logits = lax.dot_general(
            normed, router[...], (((1,), (1,)), ((), ())), preferred_element_type=F32
        )
        logits = (logits[:, :rows] + logits[:, rows : 2 * rows]) + logits[:, 2 * rows :]
        picked = jnp.where(chosen > 0.0, jax.nn.sigmoid(logits), 0.0)
        gates[unit] = picked / jnp.sum(picked, axis=-1, keepdims=True)

    def serve(unit):
        @pl.when(unit == 0)
        def _():
            for copy in weights:
                copy.wait()

        sent = slot_recv.at[unit, pl.ds(0, experts - 1)]
        pltpu.make_async_copy(sent, sent, slot_sem.at[unit]).wait()
        given = slot_recv[unit].reshape(rows, width)
        for tile in range(hidden // TILE):
            part = slice(tile * TILE, (tile + 1) * TILE)
            gate_val = jnp.dot(given, w_gate[:, part], preferred_element_type=F32)
            up_val = jnp.dot(given, w_up[:, part], preferred_element_type=F32)
            inner[:, part] = (jax.nn.silu(gate_val) * up_val).astype(BF16)
        half = width // PARTS
        for start in range(0, width, half):
            for tile in range(start, start + half, TILE):
                part = slice(tile, tile + TILE)
                answer = jnp.dot(inner[...], w_down[:, part], preferred_element_type=F32)
                back_send[unit, :, :, part] = answer.astype(BF16).reshape(experts, slots, TILE)
            for step in far_first:
                peer = (mine + step) % experts
                pltpu.make_async_remote_copy(
                    src_ref=back_send.at[unit, peer, :, pl.ds(start, half)],
                    dst_ref=back_recv.at[unit, mine, :, pl.ds(start, half)],
                    send_sem=back_send_sem,
                    recv_sem=back_sem.at[unit],
                    device_id=(section, column * experts + peer),
                    device_id_type=MESH,
                ).start()
        back_recv[unit, mine] = back_send[unit, mine]

    def combine(unit):
        sent = back_recv.at[unit, pl.ds(0, experts - 1)]
        pltpu.make_async_copy(sent, sent, back_sem.at[unit]).wait()
        answers = back_recv[unit].reshape(rows, width)
        weight = gates[unit]
        high = weight.astype(BF16)
        low = (weight - high.astype(F32)).astype(BF16)
        total = jnp.dot(high, answers, preferred_element_type=F32)
        total = total + jnp.dot(low, answers, preferred_element_type=F32)
        result[unit] = (held[unit].astype(F32) + total).astype(BF16)

        @pl.when(section < sections - 1)
        def _():
            pltpu.make_async_remote_copy(
                src_ref=result.at[unit],
                dst_ref=held.at[unit],
                send_sem=next_send_sem,
                recv_sem=held_sem.at[unit],
                device_id=(section + 1, index),
                device_id_type=MESH,
            ).start()

        batch, owner = unit // reps, unit % reps
        target = out_ref.at[0, batch, column]

        @pl.when(owner == column)
        def _():
            pltpu.make_async_copy(result.at[unit], target, out_sem).start()

        @pl.when(owner != column)
        def _():
            pltpu.make_async_remote_copy(
                src_ref=result.at[unit],
                dst_ref=target,
                send_sem=out_send_sem,
                recv_sem=out_sem,
                device_id=(section, owner * experts + mine),
                device_id_type=MESH,
            ).start()

    def at(unit, stage):
        @pl.when(jnp.logical_and(unit >= 0, unit < units))
        def _():
            stage(unit)

    def tick(now, carry):
        at(now, prepare)
        at(now - SERVE, serve)
        at(now - COMBINE, combine)
        return carry

    lax.fori_loop(0, units + COMBINE, tick, 0)

    def drain(ref, sem):
        pltpu.make_async_copy(ref, ref, sem).wait()

    drain(others, route_send_sem)
    drain(slot_send.at[:, pl.ds(0, experts - 1)], slot_send_sem)
    drain(back_send.at[:, pl.ds(0, experts - 1)], back_send_sem)

    @pl.when(section == 0)
    def _():
        drain(out_ref.at[0, :, pl.ds(0, reps - 1)], token_send_sem)

    @pl.when(section < sections - 1)
    def _():
        drain(result, next_send_sem)

    drain(out_ref.at[0, :, pl.ds(0, reps - 1)], out_send_sem)
    drain(out_ref, out_sem)


def per_device(tokens, expert_ids, router_weight, w_gate, w_up, w_down):
    micro, reps, tok, width = tokens.shape
    hidden = w_gate.shape[3]
    sections = lax.axis_size("section")
    experts = lax.axis_size("expert") // reps
    units = micro * reps
    slots = tok // 2
    rows = experts * slots
    routes = chosen_lanes(expert_ids[0])
    sizes = (sections, experts, reps, micro, tok, width, hidden)
    anywhere = pl.BlockSpec(memory_space=pl.ANY)
    local = pl.BlockSpec(memory_space=pltpu.VMEM)
    dma = pltpu.SemaphoreType.DMA
    exchange = pltpu.VMEM((units, experts, slots, width), BF16)
    return pl.pallas_call(
        functools.partial(pipeline, sizes),
        out_shape=jax.ShapeDtypeStruct((1, micro, reps, tok, width), BF16),
        in_specs=[anywhere, local, anywhere, anywhere, anywhere, anywhere],
        out_specs=anywhere,
        scratch_shapes=[
            pltpu.VMEM((width, hidden), BF16),
            pltpu.VMEM((width, hidden), BF16),
            pltpu.VMEM((hidden, width), BF16),
            pltpu.VMEM((units, tok, width), BF16),
            pltpu.VMEM((reps, tok, 128), F32),
            pltpu.VMEM((experts, width), F32),
            pltpu.VMEM((3 * rows, width), BF16),
            pltpu.VMEM((units, tok, rows), F32),
            exchange,
            exchange,
            pltpu.VMEM((rows, hidden), BF16),
            exchange,
            exchange,
            pltpu.VMEM((units, tok, width), BF16),
            dma((3,)),
            dma,
            dma,
            dma,
            dma,
            dma((units,)),
            dma((units,)),
            dma,
            dma((units,)),
            dma,
            dma,
            dma,
            dma,
        ],
        compiler_params=pltpu.CompilerParams(
            collective_id=0, has_side_effects=True, vmem_limit_bytes=52 * 1024 * 1024
        ),
    )(tokens, routes, jnp.swapaxes(router_weight[0], 1, 2), w_gate[0, 0], w_up[0, 0], w_down[0, 0])


def solution(mesh):
    in_specs = (
        P(None, None, "expert", None),
        P("section", None, None, "expert", None),
        P("section", None, None, None),
        P("section", "expert", None, None),
        P("section", "expert", None, None),
        P("section", "expert", None, None),
    )
    out_specs = P("section", None, None, "expert", None)
    return jax.shard_map(
        per_device, mesh=mesh, in_specs=in_specs, out_specs=out_specs, check_vma=False
    )
```

time: 197 us -> 173 us (0.88)
  Pallas kernels: 192 us -> 169 us
    pallas_call x1, Pallas kernels: 192 us -> 169 us  [per_device(): pl.pallas_call(functools.partial(pipeline, sizes), out_shape=jax.ShapeDty...]
where the time goes in v2:
time: 173 us
  Pallas kernels  169 us (98%)
  local copies, waits for them, and re-layouts  2.83 us (2%)
    pallas_call x1, Pallas kernels, per_device(): pl.pallas_call(functools.partial(pipeline, sizes), out_shape=jax.ShapeDty...  169 us

profile of v2, /device:TPU:231, one launch (start us, length us, event | category | flops | bytes accessed | tf_op | source)
XLA Modules:
  0.0 172.6 jit_solution(1765907857422204309)
XLA Ops:
  0.0 0.7 convert_bitcast_fusion
  0.7 0.1 copy.9
  0.8 0.0 copy-start
  0.8 1.0 copy-done
  1.9 0.0 copy-start.1
  1.9 0.9 copy-done.1
  2.8 169.0 %shard_map.64 = bf16[1,4,4,16,1024]{4,3,2,1,0:T(8,128)(2,1)S(1)} custom-call(bf16[4,4,16,1024]{3,2,1,0:T(8,128)(2,1)S(1)} %copy-done, f32[4,16,128]{2,1,0:T(8,128)S(1)} %pad.4.routes_ref, f32[4,8,1024]{2,1,0:T(8,128)S(1)} %bitcast.11, bf16[1024,1792]{1,0:T(8,128)(2,1)} %bitcast.12, bf16[1024,1792]{1,0:T(8,128)(2,1)} %bitcast.13, bf16[1792,1024]{1,0:T(8,128)(2,1)} %bitcast.14), custom_call_target="tpu_custom_call" | custom-call | tf_op jit(solution)/shard_map/pallas_call | solution.py:328
  171.8 0.8 copy.11
  (2 shorter events, 0.0 us)
Async XLA Ops:
  0.8 1.0 copy-start
  1.9 0.9 copy-start.1
